TPU v7x, 32 devices: a whole 2x2x4 slice. The times are simulated.
32 devices in a mesh: row: 4 (over x, core), col: 8 (over z, y).
Axes of the slice: x: 2, y: 2, z: 4, core: 2. Of those that a mesh axis runs over, the one named last changes fastest.
Arguments:
- stem: float32 [2, 4, 1024, 1024], P(None, 'row', 'col'), may hold values from -6 to 6
- branch: float32 [2, 1024, 1024], replicated, may hold values from -0.125 to 0.125
Outputs:
- absorbed: float32 [2, 1024, 4, 1024], P(None, ('row', 'col'))
All inputs are finite; a program needn't handle non-finite values.
Results may differ from a plain program's by a relative error of at most 0.00007.
Values sent between devices are 32-bit elements; how exact they have to be, the bound alone decides.
No kernel may reach another device: no remote copies, remote signals or barrier semaphores. Data moves between devices by JAX's collectives and lax.ppermute only.
A program may use at most 64 MiB of HBM per device.

v0:
```python
import functools

import jax
import jax.numpy as jnp
from jax import lax
from jax.experimental import pallas as pl
from jax.experimental.pallas import tpu as pltpu
from jax.sharding import Mesh, PartitionSpec as P


LANES = 128
SUBLANES = 8
STEPS = 4


COLS = ("far", "near", "side")
PLANE = ("row", "side")


def counts():
    rows_count = lax.axis_size("row")
    cols_count = 1
    for name in COLS:
        cols_count *= lax.axis_size(name)
    return rows_count, cols_count


def plain(stem, branch):
    rows_count, cols_count = counts()
    entries = stem.shape[2]
    remain = stem.shape[3]
    contract = branch.shape[1]
    opened = branch.shape[2]
    middle = entries * cols_count // contract
    owned = remain // (rows_count * cols_count)
    blocks = stem.reshape(2, 1, entries, rows_count * cols_count, owned)
    blocks = jnp.moveaxis(blocks, 3, 0)
    moved = lax.all_to_all(blocks, ("row", *COLS), 0, 0, tiled=True)
    moved = moved.reshape(rows_count, cols_count, 2, entries, owned)
    split = moved.transpose(2, 0, 1, 3, 4).reshape(
        2, rows_count, contract, middle, owned
    )
    high = lax.Precision.HIGHEST
    dot = functools.partial(jnp.einsum, "akml,ko->lamo", precision=high)
    real = dot(split[0], branch[0]) - dot(split[1], branch[1])
    imag = dot(split[0], branch[1]) + dot(split[1], branch[0])
    return jnp.stack([real, imag]).reshape(2, owned, rows_count, middle * opened)


def params(mib):
    return pltpu.CompilerParams(vmem_limit_bytes=mib << 20)


def whole():
    return pl.BlockSpec(memory_space=pltpu.VMEM)


def turned(stem_ref, r, c, width, far):
    start = pl.multiple_of((2 * r + far) * width, width)
    return stem_ref[c, 0, :, pl.ds(start, width)].T


def place(stem_ref, far, same, other):
    entries = stem_ref.shape[2]
    blocks, _, owned, _ = same.shape
    rows_count = lax.axis_size("row")
    sides = blocks // rows_count
    half = sides * owned
    here = lax.axis_index("near") == 0
    for r in range(rows_count):
        at = pl.ds(r * sides, sides)
        for c in range(2):
            whole_width = turned(stem_ref, r, c, 2 * half, far)
            low, high = whole_width[:half], whole_width[half:]
            shape = (sides, owned, entries)
            same[at, c] = jnp.where(here, low, high).reshape(shape)
            other[at, c] = jnp.where(here, high, low).reshape(shape)


def pack_far_kernel(stem_ref, first_ref, second_ref):
    place(stem_ref, 1 - lax.axis_index("far"), first_ref, second_ref)


def mine():
    return lax.axis_index("row") * lax.axis_size("side") + lax.axis_index("side")


def pack_near_kernel(stem_ref, second_ref, *refs):
    *piece_refs, beside_ref, own = refs
    place(stem_ref, lax.axis_index("far"), own, beside_ref)
    for t, piece_ref in enumerate(piece_refs):
        to = jnp.bitwise_xor(mine(), t)
        piece_ref[0] = second_ref[to]
        piece_ref[1] = own[to]


def parts_kernel(first_ref, beside_ref, *piece_refs):
    for t, piece_ref in enumerate(piece_refs):
        to = jnp.bitwise_xor(mine(), t)
        piece_ref[0] = first_ref[to]
        piece_ref[1] = beside_ref[to]


def collect_kernel(*refs):
    *piece_refs, second_ref, own_ref = refs
    for t, piece_ref in enumerate(piece_refs):
        at = jnp.bitwise_xor(mine(), t)
        second_ref[at] = piece_ref[0]
        own_ref[at] = piece_ref[1]


def small(kernel, args, outs, scratch=()):
    return pl.pallas_call(
        kernel,
        in_specs=[whole()] * len(args),
        out_specs=[whole()] * len(outs),
        out_shape=[jax.ShapeDtypeStruct(out, jnp.float32) for out in outs],
        scratch_shapes=[pltpu.VMEM(shape, jnp.float32) for shape in scratch],
        compiler_params=params(4),
    )(*args)


def halves(x):
    high = x.astype(jnp.bfloat16)
    low = (x - high.astype(jnp.float32)).astype(jnp.bfloat16)
    return high, low


def gather(moved_ref, which, gathered, both):
    blocks, _, _, owned, entries = moved_ref.shape
    rows = both.shape[0] // 4
    rows_count = rows // owned
    sides = blocks // rows_count
    for j in range(sides):
        for c in range(2):
            for r in range(rows_count):
                gathered[pl.ds(c * rows + r, owned, stride=rows_count), :] = moved_ref[
                    r * sides + j, which, c
                ]
        cols = pl.ds(j * entries, entries)
        both[: 2 * rows, cols], both[2 * rows :, cols] = halves(gathered[...])


def senders_rows(far_flip, near_flip, depth):
    far = lax.axis_index("far")
    near = lax.axis_index("near")
    far = 1 - far if far_flip else far
    near = 1 - near if near_flip else near
    return pl.ds(pl.multiple_of((2 * far + near) * depth, depth), depth)


def products(both, high, low):
    rows = both.shape[0] // 4
    dot = functools.partial(jnp.dot, preferred_element_type=jnp.float32)
    sums = []
    for c in range(2):
        wide = dot(both[...], high[c])
        fine = dot(both[: 2 * rows], low[c])
        sums.append((wide[2 * rows :] + fine) + wide[: 2 * rows])
    real = sums[0][:rows] - sums[1][rows:]
    imag = sums[1][:rows] + sums[0][rows:]
    return real, imag


def multiply(senders, branch_ref, prior_ref, acc_ref, gathered, both):
    depth = both.shape[2]
    step = acc_ref.shape[-1] // STEPS
    for n, (moved_ref, which, _) in enumerate(senders):
        gather(moved_ref, which, gathered, both.at[n])
    for i in range(STEPS):
        cols = pl.ds(i * step, step)
        total = None
        if prior_ref is not None:
            total = prior_ref[0, :, cols], prior_ref[1, :, cols]
        for n, (_, _, flips) in enumerate(senders):
            part = branch_ref[:, senders_rows(*flips, depth), cols]
            more = products(both.at[n], *halves(part))
            total = more if total is None else (total[0] + more[0], total[1] + more[1])
        acc_ref[0, :, cols], acc_ref[1, :, cols] = total


def own_kernel(own_ref, branch_ref, acc_ref, gathered, both):
    multiply([(own_ref, 0, (0, 0))], branch_ref, None, acc_ref, gathered, both)


def late_kernel(*refs):
    *piece_refs, branch_ref, prior_ref, acc_ref, gathered, both, moved = refs
    for t, piece_ref in enumerate(piece_refs):
        moved[jnp.bitwise_xor(mine(), t)] = piece_ref[...]
    senders = [(moved, 0, (1, 0)), (moved, 1, (0, 1))]
    multiply(senders, branch_ref, prior_ref, acc_ref, gathered, both)


def last_kernel(
    moved_ref, branch_ref, prior_ref, out_ref, gathered, both, result, sems
):
    gather(moved_ref, 0, gathered, both)
    _, owned, rows_count, opened = result.shape
    step = opened // STEPS
    copies = []
    for i in range(STEPS):
        cols = pl.ds(i * step, step)
        part = branch_ref[:, senders_rows(1, 1, both.shape[1]), cols]
        real, imag = products(both, *halves(part))
        shape = (owned, rows_count, step)
        result[0, :, :, cols] = (prior_ref[0, :, cols] + real).reshape(shape)
        result[1, :, :, cols] = (prior_ref[1, :, cols] + imag).reshape(shape)
        copies.append(
            pltpu.make_async_copy(
                result.at[:, :, :, cols], out_ref.at[:, :, :, cols], sems.at[i]
            )
        )
        copies[-1].start()
    for copy in copies:
        copy.wait()


def absorb(kernel, block, args, branch, prior, senders, scratch=()):
    blocks, _, owned, entries = block
    rows_count = lax.axis_size("row")
    opened = branch.shape[-1]
    rows = owned * rows_count
    depth = blocks // rows_count * entries
    args = [*args, branch] + ([] if prior is None else [prior])
    return pl.pallas_call(
        kernel,
        in_specs=[whole()] * len(args),
        out_specs=whole(),
        out_shape=jax.ShapeDtypeStruct((2, rows, opened), jnp.float32),
        scratch_shapes=[
            pltpu.VMEM((2 * rows, entries), jnp.float32),
            pltpu.VMEM((senders, 4 * rows, depth), jnp.bfloat16),
            *(pltpu.VMEM(shape, jnp.float32) for shape in scratch),
        ],
        compiler_params=params(16),
    )(*args)


def absorb_last(moved, branch, prior):
    blocks, _, _, owned, entries = moved.shape
    rows_count = lax.axis_size("row")
    opened = branch.shape[-1]
    rows = owned * rows_count
    depth = blocks // rows_count * entries
    out = (2, owned, rows_count, opened)
    return pl.pallas_call(
        last_kernel,
        in_specs=[whole()] * 3,
        out_specs=pl.BlockSpec(memory_space=pl.ANY),
        out_shape=jax.ShapeDtypeStruct(out, jnp.float32),
        scratch_shapes=[
            pltpu.VMEM((2 * rows, entries), jnp.float32),
            pltpu.VMEM((4 * rows, depth), jnp.bfloat16),
            pltpu.VMEM(out, jnp.float32),
            pltpu.SemaphoreType.DMA((STEPS,)),
        ],
        compiler_params=params(16),
        name="absorb_last",
    )(moved, branch, prior)


def over_planes(x, flip):
    count = lax.axis_size("far") * lax.axis_size("near")
    return lax.ppermute(x, ("far", "near"), [(i, i ^ flip) for i in range(count)])


def turns(plane, sides):
    def key(t):
        side, core, chip = t % sides, t // sides % 2, t // (2 * sides)
        return side == 0, side == chip == 0, core, -chip, -side

    return sorted(range(1, plane), key=key)


def per_device(stem, branch):
    rows_count, cols_count = counts()
    _, _, entries, remain = stem.shape
    _, contract, opened = branch.shape
    owned = remain // (rows_count * cols_count)
    plane = rows_count * lax.axis_size("side")
    fits = (
        entries * cols_count == contract
        and rows_count % 2 == 0
        and plane & (plane - 1) == 0
        and entries % LANES == 0
        and owned % SUBLANES == 0
        and opened % (STEPS * LANES) == 0
        and remain % (2 * LANES * rows_count) == 0
        and lax.axis_size("far") == lax.axis_size("near") == 2
    )
    if not fits:
        return plain(stem, branch)
    block = (plane, 2, owned, entries)
    piece = (2, *block[1:])

    def exchange(pieces):
        moved = list(pieces)
        for t in turns(plane, lax.axis_size("side")):
            pairs = [(i, i ^ t) for i in range(plane)]
            moved[t] = lax.ppermute(pieces[t], PLANE, pairs)
        return moved

    pairs = [(i, i) for i in range(rows_count)]
    branch = lax.ppermute(branch, "row", pairs)
    first, second = small(pack_far_kernel, (stem,), (block,) * 2)
    first = over_planes(first, 2)
    *early, beside = small(
        pack_near_kernel, (stem, second), (piece,) * plane + (block,), (block,)
    )
    beside = over_planes(beside, 1)
    early = exchange(early)
    second, own = small(collect_kernel, early, (block,) * 2)
    second = over_planes(second, 3)
    late = small(parts_kernel, (first, beside), (piece,) * plane)
    late = exchange(late)
    acc = absorb(own_kernel, block, [own[:, None]], branch, None, 1)
    moved = (plane, *piece)
    acc = absorb(late_kernel, block, late, branch, acc, 2, (moved,))
    return absorb_last(second[:, None], branch, acc)


def solution(mesh):
    rows_count, cols_count = mesh.shape["row"], mesh.shape["col"]
    parted = Mesh(
        mesh.devices.reshape(rows_count, 2, 2, cols_count // 4), ("row", *COLS)
    )
    return jax.shard_map(
        per_device,
        mesh=parted,
        in_specs=(P(None, "row", COLS, None), P()),
        out_specs=P(None, ("row", *COLS), None, None),
        check_vma=False,
    )
```

profile of v0, /device:TPU:0, one launch (start us, length us, event | category | flops | bytes accessed | tf_op | source)
XLA Modules:
  0.0 44.2 jit_solution(4273980666803546339)
XLA Ops:
  0.0 3.4 %collective-permute-start.8 = (f32[2,1024,1024]{2,1,0:T(8,128)}, f32[2,1024,1024]{2,1,0:T(8,128)S(1)}, u32[]{:S(2)}, u32[]{:S(2)}) collective-permute-start(f32[2,1024,1024]{2,1,0:T(8,128)} %param.3), channel_id=1, source_target_pairs={{0,0},{8,8},{16,16},{24,24},{1,1},{9,9},{17,17},{25,25},{2,2},{10,... | collective-permute-start | bytes 25165832 | tf_op jit(solution)/shard_map/ppermute | solution.py:304
  3.4 1.2 %copy-done = f32[2,1,128,1024]{3,2,1,0:T(8,128)S(1)} copy-done((f32[2,1,128,1024]{3,2,1,0:T(8,128)S(1)}, f32[2,1,128,1024]{3,2,1,0:T(8,128)}, u32[]{:S(2)}) %copy-start) | copy-done | bytes 1048600
  4.6 0.2 shard_map.28
  4.8 0.2 shard_map.29
  5.1 3.1 %collective-permute-start = (f32[2,2,32,128]{3,2,1,0:T(8,128)S(1)}, f32[2,2,32,128]{3,2,1,0:T(8,128)S(1)}, u32[]{:S(2)}, u32[]{:S(2)}) collective-permute-start(f32[2,2,32,128]{3,2,1,0:T(8,128)S(1)} %get-tuple-element.28), channel_id=1, source_target_pairs={{0,1},{1,0},{8,9},{9,8},{16,17},{17,16},{24,25},{25,24},{2,3},{3,2... | collective-permute-start | bytes 196616 | tf_op jit(solution)/shard_map/ppermute | solution.py:300
  8.1 0.0 collective-permute-start.1
  8.1 0.2 collective-permute-start.2
  8.3 3.0 %collective-permute-start.9 = (f32[8,2,32,128]{3,2,1,0:T(8,128)S(1)}, f32[8,2,32,128]{3,2,1,0:T(8,128)S(1)}, u32[]{:S(2)}, u32[]{:S(2)}) collective-permute-start(f32[8,2,32,128]{3,2,1,0:T(8,128)S(1)} %get-tuple-element.36), channel_id=1, source_target_pairs={{0,4},{2,6},{4,0},{6,2},{1,5},{3,7},{5,1},{7,3},{8,12},{10,14},{12... | collective-permute-start | bytes 786440 | tf_op jit(solution)/shard_map/ppermute | solution.py:264
  11.3 1.6 %collective-permute-start.10 = (f32[8,2,32,128]{3,2,1,0:T(8,128)S(1)}, f32[8,2,32,128]{3,2,1,0:T(8,128)S(1)}, u32[]{:S(2)}, u32[]{:S(2)}) collective-permute-start(f32[8,2,32,128]{3,2,1,0:T(8,128)S(1)} %get-tuple-element.37), channel_id=1, source_target_pairs={{0,2},{2,0},{4,6},{6,4},{1,3},{3,1},{5,7},{7,5},{8,10},{10,8},{12,... | collective-permute-start | bytes 786440 | tf_op jit(solution)/shard_map/ppermute | solution.py:264
  12.9 1.5 %collective-permute-start.3 = (f32[2,2,32,128]{3,2,1,0:T(8,128)S(1)}, f32[2,2,32,128]{3,2,1,0:T(8,128)S(1)}, u32[]{:S(2)}, u32[]{:S(2)}) collective-permute-start(f32[2,2,32,128]{3,2,1,0:T(8,128)S(1)} %get-tuple-element.31), channel_id=1, source_target_pairs={{0,16},{1,17},{8,24},{9,25},{16,0},{17,1},{24,8},{25,9},{2,18},{3,... | collective-permute-start | bytes 196616 | tf_op jit(solution)/shard_map/ppermute | solution.py:300
  14.4 0.0 collective-permute-done.2.refs_3_
  14.4 1.7 %collective-permute-start.4 = (f32[2,2,32,128]{3,2,1,0:T(8,128)S(1)}, f32[2,2,32,128]{3,2,1,0:T(8,128)S(1)}, u32[]{:S(2)}, u32[]{:S(2)}) collective-permute-start(f32[2,2,32,128]{3,2,1,0:T(8,128)S(1)} %get-tuple-element.32), channel_id=1, source_target_pairs={{0,17},{1,16},{8,25},{9,24},{16,1},{17,0},{24,9},{25,8},{2,19},{3,... | collective-permute-start | bytes 196616 | tf_op jit(solution)/shard_map/ppermute | solution.py:300
  16.1 1.2 %collective-permute-done.3.refs_4_ = f32[2,2,32,128]{3,2,1,0:T(8,128)S(1)} collective-permute-done((f32[2,2,32,128]{3,2,1,0:T(8,128)S(1)}, f32[2,2,32,128]{3,2,1,0:T(8,128)S(1)}, u32[]{:S(2)}, u32[]{:S(2)}) %collective-permute-start.3) | collective-permute-done | bytes 65568 | tf_op jit(solution)/shard_map/ppermute | solution.py:300
  17.2 2.3 %collective-permute-done.4.refs_5_ = f32[2,2,32,128]{3,2,1,0:T(8,128)S(1)} collective-permute-done((f32[2,2,32,128]{3,2,1,0:T(8,128)S(1)}, f32[2,2,32,128]{3,2,1,0:T(8,128)S(1)}, u32[]{:S(2)}, u32[]{:S(2)}) %collective-permute-start.4) | collective-permute-done | bytes 65568 | tf_op jit(solution)/shard_map/ppermute | solution.py:300
  19.6 0.6 %collective-permute-start.6 = (f32[2,2,32,128]{3,2,1,0:T(8,128)S(1)}, f32[2,2,32,128]{3,2,1,0:T(8,128)S(1)}, u32[]{:S(2)}, u32[]{:S(2)}) collective-permute-start(f32[2,2,32,128]{3,2,1,0:T(8,128)S(1)} %get-tuple-element.34), channel_id=1, source_target_pairs={{0,25},{1,24},{8,17},{9,16},{16,9},{17,8},{24,1},{25,0},{2,27},{3,... | collective-permute-start | bytes 196616 | tf_op jit(solution)/shard_map/ppermute | solution.py:300
  20.2 1.0 %collective-permute-done.5.refs_6_ = f32[2,2,32,128]{3,2,1,0:T(8,128)S(1)} collective-permute-done((f32[2,2,32,128]{3,2,1,0:T(8,128)S(1)}, f32[2,2,32,128]{3,2,1,0:T(8,128)S(1)}, u32[]{:S(2)}, u32[]{:S(2)}) %collective-permute-start.5) | collective-permute-done | bytes 65568 | tf_op jit(solution)/shard_map/ppermute | solution.py:300
  21.2 3.4 %collective-permute-done.6.refs_7_ = f32[2,2,32,128]{3,2,1,0:T(8,128)S(1)} collective-permute-done((f32[2,2,32,128]{3,2,1,0:T(8,128)S(1)}, f32[2,2,32,128]{3,2,1,0:T(8,128)S(1)}, u32[]{:S(2)}, u32[]{:S(2)}) %collective-permute-start.6) | collective-permute-done | bytes 65568 | tf_op jit(solution)/shard_map/ppermute | solution.py:300
  24.7 2.1 %collective-permute-start.7 = (f32[8,2,32,128]{3,2,1,0:T(8,128)S(1)}, f32[8,2,32,128]{3,2,1,0:T(8,128)S(1)}, u32[]{:S(2)}, u32[]{:S(2)}) collective-permute-start(f32[8,2,32,128]{3,2,1,0:T(8,128)S(1)} %get-tuple-element.35), channel_id=1, source_target_pairs={{0,6},{2,4},{4,2},{6,0},{1,7},{3,5},{5,3},{7,1},{8,14},{10,12},{12... | collective-permute-start | bytes 786440 | tf_op jit(solution)/shard_map/ppermute | solution.py:264
  26.8 0.0 collective-permute-done.9.first_ref
  26.8 0.0 collective-permute-done.10.beside_ref
  26.8 1.9 %collective-permute-start.11 = (f32[2,2,32,128]{3,2,1,0:T(8,128)S(1)}, f32[2,2,32,128]{3,2,1,0:T(8,128)S(1)}, u32[]{:S(2)}, u32[]{:S(2)}) collective-permute-start(f32[2,2,32,128]{3,2,1,0:T(8,128)S(1)} %get-tuple-element.39), channel_id=1, source_target_pairs={{0,1},{1,0},{8,9},{9,8},{16,17},{17,16},{24,25},{25,24},{2,3},{3,2... | collective-permute-start | bytes 196616 | tf_op jit(solution)/shard_map/ppermute | solution.py:300
  28.7 0.3 collective-permute-start.13
  29.0 2.1 %collective-permute-done.11.refs_1_ = f32[2,2,32,128]{3,2,1,0:T(8,128)S(1)} collective-permute-done((f32[2,2,32,128]{3,2,1,0:T(8,128)S(1)}, f32[2,2,32,128]{3,2,1,0:T(8,128)S(1)}, u32[]{:S(2)}, u32[]{:S(2)}) %collective-permute-start.11) | collective-permute-done | bytes 65568 | tf_op jit(solution)/shard_map/ppermute | solution.py:300
  31.1 2.1 %collective-permute-start.14 = (f32[2,2,32,128]{3,2,1,0:T(8,128)S(1)}, f32[2,2,32,128]{3,2,1,0:T(8,128)S(1)}, u32[]{:S(2)}, u32[]{:S(2)}) collective-permute-start(f32[2,2,32,128]{3,2,1,0:T(8,128)S(1)} %get-tuple-element.42), channel_id=1, source_target_pairs={{0,16},{1,17},{8,24},{9,25},{16,0},{17,1},{24,8},{25,9},{2,18},{3,... | collective-permute-start | bytes 196616 | tf_op jit(solution)/shard_map/ppermute | solution.py:300
  33.2 1.7 %collective-permute-start.15 = (f32[2,2,32,128]{3,2,1,0:T(8,128)S(1)}, f32[2,2,32,128]{3,2,1,0:T(8,128)S(1)}, u32[]{:S(2)}, u32[]{:S(2)}) collective-permute-start(f32[2,2,32,128]{3,2,1,0:T(8,128)S(1)} %get-tuple-element.43), channel_id=1, source_target_pairs={{0,17},{1,16},{8,25},{9,24},{16,1},{17,0},{24,9},{25,8},{2,19},{3,... | collective-permute-start | bytes 196616 | tf_op jit(solution)/shard_map/ppermute | solution.py:300
  35.0 0.9 %collective-permute-start.17 = (f32[2,2,32,128]{3,2,1,0:T(8,128)S(1)}, f32[2,2,32,128]{3,2,1,0:T(8,128)S(1)}, u32[]{:S(2)}, u32[]{:S(2)}) collective-permute-start(f32[2,2,32,128]{3,2,1,0:T(8,128)S(1)} %get-tuple-element.45), channel_id=1, source_target_pairs={{0,25},{1,24},{8,17},{9,16},{16,9},{17,8},{24,1},{25,0},{2,27},{3,... | collective-permute-start | bytes 196616 | tf_op jit(solution)/shard_map/ppermute | solution.py:300
  35.9 1.0 %shard_map.32.refs_9_ = f32[2,128,1024]{2,1,0:T(8,128)S(1)} custom-call(f32[8,1,2,32,128]{4,3,2,1,0:T(8,128)S(1)} %bitcast.2, f32[2,1024,1024]{2,1,0:T(8,128)S(1)} %collective-permute-done.8.branch_ref.refs_8_), custom_call_target="tpu_custom_call" | custom-call | tf_op jit(solution)/shard_map/pallas_call | solution.py:225
  36.9 1.7 %collective-permute-done.15.refs_5_ = f32[2,2,32,128]{3,2,1,0:T(8,128)S(1)} collective-permute-done((f32[2,2,32,128]{3,2,1,0:T(8,128)S(1)}, f32[2,2,32,128]{3,2,1,0:T(8,128)S(1)}, u32[]{:S(2)}, u32[]{:S(2)}) %collective-permute-start.15) | collective-permute-done | bytes 65568 | tf_op jit(solution)/shard_map/ppermute | solution.py:300
  38.6 0.1 collective-permute-done.16.refs_6_
  38.7 1.7 %collective-permute-done.17.refs_7_ = f32[2,2,32,128]{3,2,1,0:T(8,128)S(1)} collective-permute-done((f32[2,2,32,128]{3,2,1,0:T(8,128)S(1)}, f32[2,2,32,128]{3,2,1,0:T(8,128)S(1)}, u32[]{:S(2)}, u32[]{:S(2)}) %collective-permute-start.17) | collective-permute-done | bytes 65568 | tf_op jit(solution)/shard_map/ppermute | solution.py:300
  40.3 2.0 %shard_map.33.prior_ref = f32[2,128,1024]{2,1,0:T(8,128)S(1)} custom-call(f32[2,2,32,128]{3,2,1,0:T(8,128)S(1)} %get-tuple-element.38.refs_0_, f32[2,2,32,128]{3,2,1,0:T(8,128)S(1)} %collective-permute-done.11.refs_1_, f32[2,2,32,128]{3,2,1,0:T(8,128)S(1)} %collective-permute-done.12.refs_2_, f32[2,2,32,128]{3,2,1,0:T(8,128)S(1)} %collective-permute-done.13.refs_3_, ...), custom_call_target="tpu_custom_call" | custom-call | tf_op jit(solution)/shard_map/pallas_call | solution.py:225
  42.3 1.9 %absorb_last.1 = f32[2,32,4,1024]{3,2,1,0:T(4,128)} custom-call(f32[8,1,2,32,128]{4,3,2,1,0:T(8,128)S(1)} %bitcast.3, f32[2,1024,1024]{2,1,0:T(8,128)S(1)} %collective-permute-done.8.branch_ref.refs_8_, f32[2,128,1024]{2,1,0:T(8,128)S(1)} %shard_map.33.prior_ref), custom_call_target="tpu_custom_call" | custom-call | tf_op jit(solution)/shard_map/absorb_last/pallas_call | solution.py:246
  (13 shorter events, 0.1 us)
Async XLA Ops:
  0.0 35.0 %collective-permute-start.8 = (f32[2,1024,1024]{2,1,0:T(8,128)}, f32[2,1024,1024]{2,1,0:T(8,128)S(1)}, u32[]{:S(2)}, u32[]{:S(2)}) collective-permute-start(f32[2,1024,1024]{2,1,0:T(8,128)} %param.3), channel_id=1, source_target_pairs={{0,0},{8,8},{16,16},{24,24},{1,1},{9,9},{17,17},{25,25},{2,2},{10,... | collective-permute-start | bytes 25165832 | tf_op jit(solution)/shard_map/ppermute | solution.py:304
  3.4 1.2 %copy-start = (f32[2,1,128,1024]{3,2,1,0:T(8,128)S(1)}, f32[2,1,128,1024]{3,2,1,0:T(8,128)}, u32[]{:S(2)}) copy-start(f32[2,1,128,1024]{3,2,1,0:T(8,128)} %stem_ref.3) | copy-start | bytes 3145732
  5.1 6.3 %collective-permute-start = (f32[2,2,32,128]{3,2,1,0:T(8,128)S(1)}, f32[2,2,32,128]{3,2,1,0:T(8,128)S(1)}, u32[]{:S(2)}, u32[]{:S(2)}) collective-permute-start(f32[2,2,32,128]{3,2,1,0:T(8,128)S(1)} %get-tuple-element.28), channel_id=1, source_target_pairs={{0,1},{1,0},{8,9},{9,8},{16,17},{17,16},{24,25},{25,24},{2,3},{3,2... | collective-permute-start | bytes 196616 | tf_op jit(solution)/shard_map/ppermute | solution.py:300
  8.1 4.8 %collective-permute-start.1 = (f32[2,2,32,128]{3,2,1,0:T(8,128)S(1)}, f32[2,2,32,128]{3,2,1,0:T(8,128)S(1)}, u32[]{:S(2)}, u32[]{:S(2)}) collective-permute-start(f32[2,2,32,128]{3,2,1,0:T(8,128)S(1)} %get-tuple-element.29), channel_id=1, source_target_pairs={{0,8},{1,9},{8,0},{9,1},{16,24},{17,25},{24,16},{25,17},{2,10},{3,... | collective-permute-start | bytes 196616 | tf_op jit(solution)/shard_map/ppermute | solution.py:300
  8.1 6.3 %collective-permute-start.2 = (f32[2,2,32,128]{3,2,1,0:T(8,128)S(1)}, f32[2,2,32,128]{3,2,1,0:T(8,128)S(1)}, u32[]{:S(2)}, u32[]{:S(2)}) collective-permute-start(f32[2,2,32,128]{3,2,1,0:T(8,128)S(1)} %get-tuple-element.30), channel_id=1, source_target_pairs={{0,9},{1,8},{8,1},{9,0},{16,25},{17,24},{24,17},{25,16},{2,11},{3,... | collective-permute-start | bytes 196616 | tf_op jit(solution)/shard_map/ppermute | solution.py:300
  8.3 18.5 %collective-permute-start.9 = (f32[8,2,32,128]{3,2,1,0:T(8,128)S(1)}, f32[8,2,32,128]{3,2,1,0:T(8,128)S(1)}, u32[]{:S(2)}, u32[]{:S(2)}) collective-permute-start(f32[8,2,32,128]{3,2,1,0:T(8,128)S(1)} %get-tuple-element.36), channel_id=1, source_target_pairs={{0,4},{2,6},{4,0},{6,2},{1,5},{3,7},{5,1},{7,3},{8,12},{10,14},{12... | collective-permute-start | bytes 786440 | tf_op jit(solution)/shard_map/ppermute | solution.py:264
  11.3 15.4 %collective-permute-start.10 = (f32[8,2,32,128]{3,2,1,0:T(8,128)S(1)}, f32[8,2,32,128]{3,2,1,0:T(8,128)S(1)}, u32[]{:S(2)}, u32[]{:S(2)}) collective-permute-start(f32[8,2,32,128]{3,2,1,0:T(8,128)S(1)} %get-tuple-element.37), channel_id=1, source_target_pairs={{0,2},{2,0},{4,6},{6,4},{1,3},{3,1},{5,7},{7,5},{8,10},{10,8},{12,... | collective-permute-start | bytes 786440 | tf_op jit(solution)/shard_map/ppermute | solution.py:264
  12.9 4.3 %collective-permute-start.3 = (f32[2,2,32,128]{3,2,1,0:T(8,128)S(1)}, f32[2,2,32,128]{3,2,1,0:T(8,128)S(1)}, u32[]{:S(2)}, u32[]{:S(2)}) collective-permute-start(f32[2,2,32,128]{3,2,1,0:T(8,128)S(1)} %get-tuple-element.31), channel_id=1, source_target_pairs={{0,16},{1,17},{8,24},{9,25},{16,0},{17,1},{24,8},{25,9},{2,18},{3,... | collective-permute-start | bytes 196616 | tf_op jit(solution)/shard_map/ppermute | solution.py:300
  14.4 5.2 %collective-permute-start.4 = (f32[2,2,32,128]{3,2,1,0:T(8,128)S(1)}, f32[2,2,32,128]{3,2,1,0:T(8,128)S(1)}, u32[]{:S(2)}, u32[]{:S(2)}) collective-permute-start(f32[2,2,32,128]{3,2,1,0:T(8,128)S(1)} %get-tuple-element.32), channel_id=1, source_target_pairs={{0,17},{1,16},{8,25},{9,24},{16,1},{17,0},{24,9},{25,8},{2,19},{3,... | collective-permute-start | bytes 196616 | tf_op jit(solution)/shard_map/ppermute | solution.py:300
  17.2 4.0 %collective-permute-start.5 = (f32[2,2,32,128]{3,2,1,0:T(8,128)S(1)}, f32[2,2,32,128]{3,2,1,0:T(8,128)S(1)}, u32[]{:S(2)}, u32[]{:S(2)}) collective-permute-start(f32[2,2,32,128]{3,2,1,0:T(8,128)S(1)} %get-tuple-element.33), channel_id=1, source_target_pairs={{0,24},{1,25},{8,16},{9,17},{16,8},{17,9},{24,0},{25,1},{2,26},{3,... | collective-permute-start | bytes 196616 | tf_op jit(solution)/shard_map/ppermute | solution.py:300
  19.6 5.1 %collective-permute-start.6 = (f32[2,2,32,128]{3,2,1,0:T(8,128)S(1)}, f32[2,2,32,128]{3,2,1,0:T(8,128)S(1)}, u32[]{:S(2)}, u32[]{:S(2)}) collective-permute-start(f32[2,2,32,128]{3,2,1,0:T(8,128)S(1)} %get-tuple-element.34), channel_id=1, source_target_pairs={{0,25},{1,24},{8,17},{9,16},{16,9},{17,8},{24,1},{25,0},{2,27},{3,... | collective-permute-start | bytes 196616 | tf_op jit(solution)/shard_map/ppermute | solution.py:300
  24.7 17.6 %collective-permute-start.7 = (f32[8,2,32,128]{3,2,1,0:T(8,128)S(1)}, f32[8,2,32,128]{3,2,1,0:T(8,128)S(1)}, u32[]{:S(2)}, u32[]{:S(2)}) collective-permute-start(f32[8,2,32,128]{3,2,1,0:T(8,128)S(1)} %get-tuple-element.35), channel_id=1, source_target_pairs={{0,6},{2,4},{4,2},{6,0},{1,7},{3,5},{5,3},{7,1},{8,14},{10,12},{12... | collective-permute-start | bytes 786440 | tf_op jit(solution)/shard_map/ppermute | solution.py:264
  26.8 4.3 %collective-permute-start.11 = (f32[2,2,32,128]{3,2,1,0:T(8,128)S(1)}, f32[2,2,32,128]{3,2,1,0:T(8,128)S(1)}, u32[]{:S(2)}, u32[]{:S(2)}) collective-permute-start(f32[2,2,32,128]{3,2,1,0:T(8,128)S(1)} %get-tuple-element.39), channel_id=1, source_target_pairs={{0,1},{1,0},{8,9},{9,8},{16,17},{17,16},{24,25},{25,24},{2,3},{3,2... | collective-permute-start | bytes 196616 | tf_op jit(solution)/shard_map/ppermute | solution.py:300
  28.7 4.5 %collective-permute-start.12 = (f32[2,2,32,128]{3,2,1,0:T(8,128)S(1)}, f32[2,2,32,128]{3,2,1,0:T(8,128)S(1)}, u32[]{:S(2)}, u32[]{:S(2)}) collective-permute-start(f32[2,2,32,128]{3,2,1,0:T(8,128)S(1)} %get-tuple-element.40), channel_id=1, source_target_pairs={{0,8},{1,9},{8,0},{9,1},{16,24},{17,25},{24,16},{25,17},{2,10},{3,... | collective-permute-start | bytes 196616 | tf_op jit(solution)/shard_map/ppermute | solution.py:300
  28.7 6.3 %collective-permute-start.13 = (f32[2,2,32,128]{3,2,1,0:T(8,128)S(1)}, f32[2,2,32,128]{3,2,1,0:T(8,128)S(1)}, u32[]{:S(2)}, u32[]{:S(2)}) collective-permute-start(f32[2,2,32,128]{3,2,1,0:T(8,128)S(1)} %get-tuple-element.41), channel_id=1, source_target_pairs={{0,9},{1,8},{8,1},{9,0},{16,25},{17,24},{24,17},{25,16},{2,11},{3,... | collective-permute-start | bytes 196616 | tf_op jit(solution)/shard_map/ppermute | solution.py:300
  31.1 5.8 %collective-permute-start.14 = (f32[2,2,32,128]{3,2,1,0:T(8,128)S(1)}, f32[2,2,32,128]{3,2,1,0:T(8,128)S(1)}, u32[]{:S(2)}, u32[]{:S(2)}) collective-permute-start(f32[2,2,32,128]{3,2,1,0:T(8,128)S(1)} %get-tuple-element.42), channel_id=1, source_target_pairs={{0,16},{1,17},{8,24},{9,25},{16,0},{17,1},{24,8},{25,9},{2,18},{3,... | collective-permute-start | bytes 196616 | tf_op jit(solution)/shard_map/ppermute | solution.py:300
  33.2 5.4 %collective-permute-start.15 = (f32[2,2,32,128]{3,2,1,0:T(8,128)S(1)}, f32[2,2,32,128]{3,2,1,0:T(8,128)S(1)}, u32[]{:S(2)}, u32[]{:S(2)}) collective-permute-start(f32[2,2,32,128]{3,2,1,0:T(8,128)S(1)} %get-tuple-element.43), channel_id=1, source_target_pairs={{0,17},{1,16},{8,25},{9,24},{16,1},{17,0},{24,9},{25,8},{2,19},{3,... | collective-permute-start | bytes 196616 | tf_op jit(solution)/shard_map/ppermute | solution.py:300
  35.0 3.7 %collective-permute-start.16 = (f32[2,2,32,128]{3,2,1,0:T(8,128)S(1)}, f32[2,2,32,128]{3,2,1,0:T(8,128)S(1)}, u32[]{:S(2)}, u32[]{:S(2)}) collective-permute-start(f32[2,2,32,128]{3,2,1,0:T(8,128)S(1)} %get-tuple-element.44), channel_id=1, source_target_pairs={{0,24},{1,25},{8,16},{9,17},{16,8},{17,9},{24,0},{25,1},{2,26},{3,... | collective-permute-start | bytes 196616 | tf_op jit(solution)/shard_map/ppermute | solution.py:300
  35.0 5.4 %collective-permute-start.17 = (f32[2,2,32,128]{3,2,1,0:T(8,128)S(1)}, f32[2,2,32,128]{3,2,1,0:T(8,128)S(1)}, u32[]{:S(2)}, u32[]{:S(2)}) collective-permute-start(f32[2,2,32,128]{3,2,1,0:T(8,128)S(1)} %get-tuple-element.45), channel_id=1, source_target_pairs={{0,25},{1,24},{8,17},{9,16},{16,9},{17,8},{24,1},{25,0},{2,27},{3,... | collective-permute-start | bytes 196616 | tf_op jit(solution)/shard_map/ppermute | solution.py:300
where the time goes:
time: 44.4 us; the launch traced here: 44.2 us
  starting transfers between devices  24 us (54%)
  waiting for transfers between devices  13.5 us (30%)
  Pallas kernels  5.36 us (12%)
  local copies, waits for them, and re-layouts  1.22 us (3%)
    ppermute x14, starting transfers between devices, exchange(): moved[t] = lax.ppermute(pieces[t], PLANE, pairs)  14 us
    ppermute x14, waiting for transfers between devices, exchange(): moved[t] = lax.ppermute(pieces[t], PLANE, pairs)  13.5 us
    ppermute x3, starting transfers between devices, over_planes(): lax.ppermute(x, ('far', 'near'), [(i, i ^ flip) for i in range(count)])  6.66 us
    ppermute x1, starting transfers between devices, per_device(): branch = lax.ppermute(branch, 'row', pairs)  3.38 us
    pallas_call x2, Pallas kernels, absorb(): pl.pallas_call(kernel, in_specs=[whole()] * len(args), out_specs=whole(),...  2.97 us
    pallas_call x1, Pallas kernels, absorb_last(): pl.pallas_call(last_kernel, in_specs=[whole()] * 3, out_specs=pl.BlockSpe...  1.88 us
    unnamed x2, local copies, waits for them, and re-layouts  1.22 us
  transfers between devices with their start and end apart: 18, of which 8 were waited for; matrix products, arithmetic and copies ran while one was open for 0% of the time, Pallas kernels for 8%

commit v1 on v0

--- a/solution.py
+++ b/solution.py
@@ -183,12 +183,35 @@
     multiply([(own_ref, 0, (0, 0))], branch_ref, None, acc_ref, gathered, both)
 
 
-def late_kernel(*refs):
+def late_kernel(group, *refs):
     *piece_refs, branch_ref, prior_ref, acc_ref, gathered, both, moved = refs
-    for t, piece_ref in enumerate(piece_refs):
-        moved[jnp.bitwise_xor(mine(), t)] = piece_ref[...]
-    senders = [(moved, 0, (1, 0)), (moved, 1, (0, 1))]
-    multiply(senders, branch_ref, prior_ref, acc_ref, gathered, both)
+    rows_count, _, _, owned, entries = moved.shape
+    rows = rows_count * owned
+    sides = lax.axis_size("side")
+    for n, piece_ref in enumerate(piece_refs):
+        moved[jnp.bitwise_xor(lax.axis_index("row"), n)] = piece_ref[...]
+    far, near = lax.axis_index("far"), lax.axis_index("near")
+    side = jnp.bitwise_xor(lax.axis_index("side"), group)
+    places = (2 * (1 - far) + near, 2 * far + 1 - near)
+    starts = [
+        pl.multiple_of((place_ * sides + side) * entries, entries) for place_ in places
+    ]
+    for which in range(2):
+        for c in range(2):
+            for r in range(rows_count):
+                gathered[pl.ds(c * rows + r, owned, stride=rows_count), :] = moved[
+                    r, which, c
+                ]
+        cols = pl.ds(which * entries, entries)
+        both[: 2 * rows, cols], both[2 * rows :, cols] = halves(gathered[...])
+    step = acc_ref.shape[-1] // STEPS
+    for i in range(STEPS):
+        cols = pl.ds(i * step, step)
+        parts = [halves(branch_ref[:, pl.ds(start, entries), cols]) for start in starts]
+        high, low = (jnp.concatenate(part, axis=1) for part in zip(*parts))
+        real, imag = products(both, high, low)
+        acc_ref[0, :, cols] = prior_ref[0, :, cols] + real
+        acc_ref[1, :, cols] = prior_ref[1, :, cols] + imag
 
 
 def last_kernel(
@@ -215,12 +238,11 @@
         copy.wait()
 
 
-def absorb(kernel, block, args, branch, prior, senders, scratch=()):
-    blocks, _, owned, entries = block
+def absorb(kernel, block, args, branch, prior, both, scratch=()):
+    _, _, owned, entries = block
     rows_count = lax.axis_size("row")
     opened = branch.shape[-1]
     rows = owned * rows_count
-    depth = blocks // rows_count * entries
     args = [*args, branch] + ([] if prior is None else [prior])
     return pl.pallas_call(
         kernel,
@@ -229,7 +251,7 @@
         out_shape=jax.ShapeDtypeStruct((2, rows, opened), jnp.float32),
         scratch_shapes=[
             pltpu.VMEM((2 * rows, entries), jnp.float32),
-            pltpu.VMEM((senders, 4 * rows, depth), jnp.bfloat16),
+            pltpu.VMEM(both, jnp.bfloat16),
             *(pltpu.VMEM(shape, jnp.float32) for shape in scratch),
         ],
         compiler_params=params(16),
@@ -267,7 +289,7 @@
 def turns(plane, sides):
     def key(t):
         side, core, chip = t % sides, t // sides % 2, t // (2 * sides)
-        return side == 0, side == chip == 0, core, -chip, -side
+        return 5 * (side == 0) + 4 * core + 2 * (chip == 0), -chip, -side
 
     return sorted(range(1, plane), key=key)
 
@@ -313,9 +335,20 @@
     second = over_planes(second, 3)
     late = small(parts_kernel, (first, beside), (piece,) * plane)
     late = exchange(late)
-    acc = absorb(own_kernel, block, [own[:, None]], branch, None, 1)
-    moved = (plane, *piece)
-    acc = absorb(late_kernel, block, late, branch, acc, 2, (moved,))
+    sides = lax.axis_size("side")
+    rows = 4 * owned * rows_count
+    both = (1, rows, sides * entries)
+    acc = absorb(own_kernel, block, [own[:, None]], branch, None, both)
+    for group in range(sides - 1, -1, -1):
+        acc = absorb(
+            functools.partial(late_kernel, group),
+            block,
+            late[group::sides],
+            branch,
+            acc,
+            (rows, 2 * entries),
+            ((rows_count, *piece),),
+        )
     return absorb_last(second[:, None], branch, acc)
 
 

time: 44.4 us -> 44.1 us (level)
    pallas_call x2 -> x3, Pallas kernels: 2.97 us -> 3.13 us  [absorb(): pl.pallas_call(kernel, in_specs=[whole()] * len(args), out_specs=whole(),...]
where the time goes in v1:
time: 44.1 us; the launch traced here: 43.9 us
  starting transfers between devices  23.8 us (54%)
  waiting for transfers between devices  13.2 us (30%)
  Pallas kernels  5.52 us (13%)
  local copies, waits for them, and re-layouts  1.22 us (3%)
    ppermute x14, starting transfers between devices, exchange(): moved[t] = lax.ppermute(pieces[t], PLANE, pairs)  13.8 us
    ppermute x14, waiting for transfers between devices, exchange(): moved[t] = lax.ppermute(pieces[t], PLANE, pairs)  13.2 us
    ppermute x3, starting transfers between devices, over_planes(): lax.ppermute(x, ('far', 'near'), [(i, i ^ flip) for i in range(count)])  6.66 us
    ppermute x1, starting transfers between devices, per_device(): branch = lax.ppermute(branch, 'row', pairs)  3.38 us
    pallas_call x3, Pallas kernels, absorb(): pl.pallas_call(kernel, in_specs=[whole()] * len(args), out_specs=whole(),...  3.13 us
    pallas_call x1, Pallas kernels, absorb_last(): pl.pallas_call(last_kernel, in_specs=[whole()] * 3, out_specs=pl.BlockSpe...  1.88 us
    unnamed x2, local copies, waits for them, and re-layouts  1.22 us
  transfers between devices with their start and end apart: 18, of which 8 were waited for; matrix products, arithmetic and copies ran while one was open for 0% of the time, Pallas kernels for 8%

profile of v1, /device:TPU:0, one launch (start us, length us, event | category | flops | bytes accessed | tf_op | source)
XLA Modules:
  0.0 43.9 jit_solution(17823175043714273757)
XLA Ops:
  0.0 3.4 %collective-permute-start.8 = (f32[2,1024,1024]{2,1,0:T(8,128)}, f32[2,1024,1024]{2,1,0:T(8,128)S(1)}, u32[]{:S(2)}, u32[]{:S(2)}) collective-permute-start(f32[2,1024,1024]{2,1,0:T(8,128)} %param.3), channel_id=1, source_target_pairs={{0,0},{8,8},{16,16},{24,24},{1,1},{9,9},{17,17},{25,25},{2,2},{10,... | collective-permute-start | bytes 25165832 | tf_op jit(solution)/shard_map/ppermute | solution.py:326
  3.4 1.2 %copy-done = f32[2,1,128,1024]{3,2,1,0:T(8,128)S(1)} copy-done((f32[2,1,128,1024]{3,2,1,0:T(8,128)S(1)}, f32[2,1,128,1024]{3,2,1,0:T(8,128)}, u32[]{:S(2)}) %copy-start) | copy-done | bytes 1048600
  4.6 0.2 shard_map.28
  4.8 0.2 shard_map.29
  5.1 3.1 %collective-permute-start = (f32[2,2,32,128]{3,2,1,0:T(8,128)S(1)}, f32[2,2,32,128]{3,2,1,0:T(8,128)S(1)}, u32[]{:S(2)}, u32[]{:S(2)}) collective-permute-start(f32[2,2,32,128]{3,2,1,0:T(8,128)S(1)} %get-tuple-element.28), channel_id=1, source_target_pairs={{0,1},{1,0},{8,9},{9,8},{16,17},{17,16},{24,25},{25,24},{2,3},{3,2... | collective-permute-start | bytes 196616 | tf_op jit(solution)/shard_map/ppermute | solution.py:322
  8.1 0.0 collective-permute-start.1
  8.1 0.2 collective-permute-start.2
  8.3 3.0 %collective-permute-start.9 = (f32[8,2,32,128]{3,2,1,0:T(8,128)S(1)}, f32[8,2,32,128]{3,2,1,0:T(8,128)S(1)}, u32[]{:S(2)}, u32[]{:S(2)}) collective-permute-start(f32[8,2,32,128]{3,2,1,0:T(8,128)S(1)} %get-tuple-element.36), channel_id=1, source_target_pairs={{0,4},{2,6},{4,0},{6,2},{1,5},{3,7},{5,1},{7,3},{8,12},{10,14},{12... | collective-permute-start | bytes 786440 | tf_op jit(solution)/shard_map/ppermute | solution.py:286
  11.3 1.6 %collective-permute-start.10 = (f32[8,2,32,128]{3,2,1,0:T(8,128)S(1)}, f32[8,2,32,128]{3,2,1,0:T(8,128)S(1)}, u32[]{:S(2)}, u32[]{:S(2)}) collective-permute-start(f32[8,2,32,128]{3,2,1,0:T(8,128)S(1)} %get-tuple-element.37), channel_id=1, source_target_pairs={{0,2},{2,0},{4,6},{6,4},{1,3},{3,1},{5,7},{7,5},{8,10},{10,8},{12,... | collective-permute-start | bytes 786440 | tf_op jit(solution)/shard_map/ppermute | solution.py:286
  12.9 1.5 %collective-permute-start.3 = (f32[2,2,32,128]{3,2,1,0:T(8,128)S(1)}, f32[2,2,32,128]{3,2,1,0:T(8,128)S(1)}, u32[]{:S(2)}, u32[]{:S(2)}) collective-permute-start(f32[2,2,32,128]{3,2,1,0:T(8,128)S(1)} %get-tuple-element.31), channel_id=1, source_target_pairs={{0,16},{1,17},{8,24},{9,25},{16,0},{17,1},{24,8},{25,9},{2,18},{3,... | collective-permute-start | bytes 196616 | tf_op jit(solution)/shard_map/ppermute | solution.py:322
  14.4 0.0 collective-permute-done.2.refs_3_
  14.4 1.7 %collective-permute-start.4 = (f32[2,2,32,128]{3,2,1,0:T(8,128)S(1)}, f32[2,2,32,128]{3,2,1,0:T(8,128)S(1)}, u32[]{:S(2)}, u32[]{:S(2)}) collective-permute-start(f32[2,2,32,128]{3,2,1,0:T(8,128)S(1)} %get-tuple-element.32), channel_id=1, source_target_pairs={{0,17},{1,16},{8,25},{9,24},{16,1},{17,0},{24,9},{25,8},{2,19},{3,... | collective-permute-start | bytes 196616 | tf_op jit(solution)/shard_map/ppermute | solution.py:322
  16.1 1.2 %collective-permute-done.3.refs_4_ = f32[2,2,32,128]{3,2,1,0:T(8,128)S(1)} collective-permute-done((f32[2,2,32,128]{3,2,1,0:T(8,128)S(1)}, f32[2,2,32,128]{3,2,1,0:T(8,128)S(1)}, u32[]{:S(2)}, u32[]{:S(2)}) %collective-permute-start.3) | collective-permute-done | bytes 65568 | tf_op jit(solution)/shard_map/ppermute | solution.py:322
  17.2 2.3 %collective-permute-done.4.refs_5_ = f32[2,2,32,128]{3,2,1,0:T(8,128)S(1)} collective-permute-done((f32[2,2,32,128]{3,2,1,0:T(8,128)S(1)}, f32[2,2,32,128]{3,2,1,0:T(8,128)S(1)}, u32[]{:S(2)}, u32[]{:S(2)}) %collective-permute-start.4) | collective-permute-done | bytes 65568 | tf_op jit(solution)/shard_map/ppermute | solution.py:322
  19.6 0.6 %collective-permute-start.6 = (f32[2,2,32,128]{3,2,1,0:T(8,128)S(1)}, f32[2,2,32,128]{3,2,1,0:T(8,128)S(1)}, u32[]{:S(2)}, u32[]{:S(2)}) collective-permute-start(f32[2,2,32,128]{3,2,1,0:T(8,128)S(1)} %get-tuple-element.34), channel_id=1, source_target_pairs={{0,25},{1,24},{8,17},{9,16},{16,9},{17,8},{24,1},{25,0},{2,27},{3,... | collective-permute-start | bytes 196616 | tf_op jit(solution)/shard_map/ppermute | solution.py:322
  20.2 1.0 %collective-permute-done.5.refs_6_ = f32[2,2,32,128]{3,2,1,0:T(8,128)S(1)} collective-permute-done((f32[2,2,32,128]{3,2,1,0:T(8,128)S(1)}, f32[2,2,32,128]{3,2,1,0:T(8,128)S(1)}, u32[]{:S(2)}, u32[]{:S(2)}) %collective-permute-start.5) | collective-permute-done | bytes 65568 | tf_op jit(solution)/shard_map/ppermute | solution.py:322
  21.2 3.4 %collective-permute-done.6.refs_7_ = f32[2,2,32,128]{3,2,1,0:T(8,128)S(1)} collective-permute-done((f32[2,2,32,128]{3,2,1,0:T(8,128)S(1)}, f32[2,2,32,128]{3,2,1,0:T(8,128)S(1)}, u32[]{:S(2)}, u32[]{:S(2)}) %collective-permute-start.6) | collective-permute-done | bytes 65568 | tf_op jit(solution)/shard_map/ppermute | solution.py:322
  24.7 2.1 %collective-permute-start.7 = (f32[8,2,32,128]{3,2,1,0:T(8,128)S(1)}, f32[8,2,32,128]{3,2,1,0:T(8,128)S(1)}, u32[]{:S(2)}, u32[]{:S(2)}) collective-permute-start(f32[8,2,32,128]{3,2,1,0:T(8,128)S(1)} %get-tuple-element.35), channel_id=1, source_target_pairs={{0,6},{2,4},{4,2},{6,0},{1,7},{3,5},{5,3},{7,1},{8,14},{10,12},{12... | collective-permute-start | bytes 786440 | tf_op jit(solution)/shard_map/ppermute | solution.py:286
  26.8 0.0 collective-permute-done.9.first_ref
  26.8 0.0 collective-permute-done.10.beside_ref
  26.8 1.9 %collective-permute-start.14 = (f32[2,2,32,128]{3,2,1,0:T(8,128)S(1)}, f32[2,2,32,128]{3,2,1,0:T(8,128)S(1)}, u32[]{:S(2)}, u32[]{:S(2)}) collective-permute-start(f32[2,2,32,128]{3,2,1,0:T(8,128)S(1)} %get-tuple-element.42), channel_id=1, source_target_pairs={{0,1},{1,0},{8,9},{9,8},{16,17},{17,16},{24,25},{25,24},{2,3},{3,2... | collective-permute-start | bytes 196616 | tf_op jit(solution)/shard_map/ppermute | solution.py:322
  28.7 1.2 %collective-permute-start.16 = (f32[2,2,32,128]{3,2,1,0:T(8,128)S(1)}, f32[2,2,32,128]{3,2,1,0:T(8,128)S(1)}, u32[]{:S(2)}, u32[]{:S(2)}) collective-permute-start(f32[2,2,32,128]{3,2,1,0:T(8,128)S(1)} %get-tuple-element.44), channel_id=1, source_target_pairs={{0,17},{1,16},{8,25},{9,24},{16,1},{17,0},{24,9},{25,8},{2,19},{3,... | collective-permute-start | bytes 196616 | tf_op jit(solution)/shard_map/ppermute | solution.py:322
  29.9 1.2 %collective-permute-done.14.refs_0_ = f32[2,2,32,128]{3,2,1,0:T(8,128)S(1)} collective-permute-done((f32[2,2,32,128]{3,2,1,0:T(8,128)S(1)}, f32[2,2,32,128]{3,2,1,0:T(8,128)S(1)}, u32[]{:S(2)}, u32[]{:S(2)}) %collective-permute-start.14) | collective-permute-done | bytes 65568 | tf_op jit(solution)/shard_map/ppermute | solution.py:322
  31.2 1.8 %collective-permute-done.15.refs_1_ = f32[2,2,32,128]{3,2,1,0:T(8,128)S(1)} collective-permute-done((f32[2,2,32,128]{3,2,1,0:T(8,128)S(1)}, f32[2,2,32,128]{3,2,1,0:T(8,128)S(1)}, u32[]{:S(2)}, u32[]{:S(2)}) %collective-permute-start.15) | collective-permute-done | bytes 65568 | tf_op jit(solution)/shard_map/ppermute | solution.py:322
  33.0 1.1 %collective-permute-start.17 = (f32[2,2,32,128]{3,2,1,0:T(8,128)S(1)}, f32[2,2,32,128]{3,2,1,0:T(8,128)S(1)}, u32[]{:S(2)}, u32[]{:S(2)}) collective-permute-start(f32[2,2,32,128]{3,2,1,0:T(8,128)S(1)} %get-tuple-element.45), channel_id=1, source_target_pairs={{0,25},{1,24},{8,17},{9,16},{16,9},{17,8},{24,1},{25,0},{2,27},{3,... | collective-permute-start | bytes 196616 | tf_op jit(solution)/shard_map/ppermute | solution.py:322
  34.1 2.5 %collective-permute-start.12 = (f32[2,2,32,128]{3,2,1,0:T(8,128)S(1)}, f32[2,2,32,128]{3,2,1,0:T(8,128)S(1)}, u32[]{:S(2)}, u32[]{:S(2)}) collective-permute-start(f32[2,2,32,128]{3,2,1,0:T(8,128)S(1)} %get-tuple-element.40), channel_id=1, source_target_pairs={{0,16},{1,17},{8,24},{9,25},{16,0},{17,1},{24,8},{25,9},{2,18},{3,... | collective-permute-start | bytes 196616 | tf_op jit(solution)/shard_map/ppermute | solution.py:322
  36.6 1.0 %shard_map.32.refs_5_ = f32[2,128,1024]{2,1,0:T(8,128)S(1)} custom-call(f32[8,1,2,32,128]{4,3,2,1,0:T(8,128)S(1)} %bitcast.2, f32[2,1024,1024]{2,1,0:T(8,128)S(1)} %collective-permute-done.8.branch_ref.refs_4_), custom_call_target="tpu_custom_call" | custom-call | tf_op jit(solution)/shard_map/pallas_call | solution.py:247
  37.6 1.1 %shard_map.33.refs_5_ = f32[2,128,1024]{2,1,0:T(8,128)S(1)} custom-call(f32[2,2,32,128]{3,2,1,0:T(8,128)S(1)} %collective-permute-done.14.refs_0_, f32[2,2,32,128]{3,2,1,0:T(8,128)S(1)} %collective-permute-done.15.refs_1_, f32[2,2,32,128]{3,2,1,0:T(8,128)S(1)} %collective-permute-done.16.refs_2_, f32[2,2,32,128]{3,2,1,0:T(8,128)S(1)} %collective-permute-done.17.refs_3_, ...), custom_call_target="tpu_custom_call" | custom-call | tf_op jit(solution)/shard_map/pallas_call | solution.py:247
  38.7 0.8 %collective-permute-done.12.refs_2_ = f32[2,2,32,128]{3,2,1,0:T(8,128)S(1)} collective-permute-done((f32[2,2,32,128]{3,2,1,0:T(8,128)S(1)}, f32[2,2,32,128]{3,2,1,0:T(8,128)S(1)}, u32[]{:S(2)}, u32[]{:S(2)}) %collective-permute-start.12) | collective-permute-done | bytes 65568 | tf_op jit(solution)/shard_map/ppermute | solution.py:322
  39.5 1.4 %collective-permute-done.13.refs_3_ = f32[2,2,32,128]{3,2,1,0:T(8,128)S(1)} collective-permute-done((f32[2,2,32,128]{3,2,1,0:T(8,128)S(1)}, f32[2,2,32,128]{3,2,1,0:T(8,128)S(1)}, u32[]{:S(2)}, u32[]{:S(2)}) %collective-permute-start.13) | collective-permute-done | bytes 65568 | tf_op jit(solution)/shard_map/ppermute | solution.py:322
  40.9 1.0 %shard_map.34.prior_ref = f32[2,128,1024]{2,1,0:T(8,128)S(1)} custom-call(f32[2,2,32,128]{3,2,1,0:T(8,128)S(1)} %get-tuple-element.38.refs_0_, f32[2,2,32,128]{3,2,1,0:T(8,128)S(1)} %collective-permute-done.11.refs_1_, f32[2,2,32,128]{3,2,1,0:T(8,128)S(1)} %collective-permute-done.12.refs_2_, f32[2,2,32,128]{3,2,1,0:T(8,128)S(1)} %collective-permute-done.13.refs_3_, ...), custom_call_target="tpu_custom_call" | custom-call | tf_op jit(solution)/shard_map/pallas_call | solution.py:247
  42.0 1.9 %absorb_last.1 = f32[2,32,4,1024]{3,2,1,0:T(4,128)} custom-call(f32[8,1,2,32,128]{4,3,2,1,0:T(8,128)S(1)} %bitcast.3, f32[2,1024,1024]{2,1,0:T(8,128)S(1)} %collective-permute-done.8.branch_ref.refs_4_, f32[2,128,1024]{2,1,0:T(8,128)S(1)} %shard_map.34.prior_ref), custom_call_target="tpu_custom_call" | custom-call | tf_op jit(solution)/shard_map/absorb_last/pallas_call | solution.py:268
  (14 shorter events, 0.1 us)
Async XLA Ops:
  0.0 36.6 %collective-permute-start.8 = (f32[2,1024,1024]{2,1,0:T(8,128)}, f32[2,1024,1024]{2,1,0:T(8,128)S(1)}, u32[]{:S(2)}, u32[]{:S(2)}) collective-permute-start(f32[2,1024,1024]{2,1,0:T(8,128)} %param.3), channel_id=1, source_target_pairs={{0,0},{8,8},{16,16},{24,24},{1,1},{9,9},{17,17},{25,25},{2,2},{10,... | collective-permute-start | bytes 25165832 | tf_op jit(solution)/shard_map/ppermute | solution.py:326
  3.4 1.2 %copy-start = (f32[2,1,128,1024]{3,2,1,0:T(8,128)S(1)}, f32[2,1,128,1024]{3,2,1,0:T(8,128)}, u32[]{:S(2)}) copy-start(f32[2,1,128,1024]{3,2,1,0:T(8,128)} %stem_ref.3) | copy-start | bytes 3145732
  5.1 6.3 %collective-permute-start = (f32[2,2,32,128]{3,2,1,0:T(8,128)S(1)}, f32[2,2,32,128]{3,2,1,0:T(8,128)S(1)}, u32[]{:S(2)}, u32[]{:S(2)}) collective-permute-start(f32[2,2,32,128]{3,2,1,0:T(8,128)S(1)} %get-tuple-element.28), channel_id=1, source_target_pairs={{0,1},{1,0},{8,9},{9,8},{16,17},{17,16},{24,25},{25,24},{2,3},{3,2... | collective-permute-start | bytes 196616 | tf_op jit(solution)/shard_map/ppermute | solution.py:322
  8.1 4.8 %collective-permute-start.1 = (f32[2,2,32,128]{3,2,1,0:T(8,128)S(1)}, f32[2,2,32,128]{3,2,1,0:T(8,128)S(1)}, u32[]{:S(2)}, u32[]{:S(2)}) collective-permute-start(f32[2,2,32,128]{3,2,1,0:T(8,128)S(1)} %get-tuple-element.29), channel_id=1, source_target_pairs={{0,8},{1,9},{8,0},{9,1},{16,24},{17,25},{24,16},{25,17},{2,10},{3,... | collective-permute-start | bytes 196616 | tf_op jit(solution)/shard_map/ppermute | solution.py:322
  8.1 6.3 %collective-permute-start.2 = (f32[2,2,32,128]{3,2,1,0:T(8,128)S(1)}, f32[2,2,32,128]{3,2,1,0:T(8,128)S(1)}, u32[]{:S(2)}, u32[]{:S(2)}) collective-permute-start(f32[2,2,32,128]{3,2,1,0:T(8,128)S(1)} %get-tuple-element.30), channel_id=1, source_target_pairs={{0,9},{1,8},{8,1},{9,0},{16,25},{17,24},{24,17},{25,16},{2,11},{3,... | collective-permute-start | bytes 196616 | tf_op jit(solution)/shard_map/ppermute | solution.py:322
  8.3 18.5 %collective-permute-start.9 = (f32[8,2,32,128]{3,2,1,0:T(8,128)S(1)}, f32[8,2,32,128]{3,2,1,0:T(8,128)S(1)}, u32[]{:S(2)}, u32[]{:S(2)}) collective-permute-start(f32[8,2,32,128]{3,2,1,0:T(8,128)S(1)} %get-tuple-element.36), channel_id=1, source_target_pairs={{0,4},{2,6},{4,0},{6,2},{1,5},{3,7},{5,1},{7,3},{8,12},{10,14},{12... | collective-permute-start | bytes 786440 | tf_op jit(solution)/shard_map/ppermute | solution.py:286
  11.3 15.4 %collective-permute-start.10 = (f32[8,2,32,128]{3,2,1,0:T(8,128)S(1)}, f32[8,2,32,128]{3,2,1,0:T(8,128)S(1)}, u32[]{:S(2)}, u32[]{:S(2)}) collective-permute-start(f32[8,2,32,128]{3,2,1,0:T(8,128)S(1)} %get-tuple-element.37), channel_id=1, source_target_pairs={{0,2},{2,0},{4,6},{6,4},{1,3},{3,1},{5,7},{7,5},{8,10},{10,8},{12,... | collective-permute-start | bytes 786440 | tf_op jit(solution)/shard_map/ppermute | solution.py:286
  12.9 4.3 %collective-permute-start.3 = (f32[2,2,32,128]{3,2,1,0:T(8,128)S(1)}, f32[2,2,32,128]{3,2,1,0:T(8,128)S(1)}, u32[]{:S(2)}, u32[]{:S(2)}) collective-permute-start(f32[2,2,32,128]{3,2,1,0:T(8,128)S(1)} %get-tuple-element.31), channel_id=1, source_target_pairs={{0,16},{1,17},{8,24},{9,25},{16,0},{17,1},{24,8},{25,9},{2,18},{3,... | collective-permute-start | bytes 196616 | tf_op jit(solution)/shard_map/ppermute | solution.py:322
  14.4 5.2 %collective-permute-start.4 = (f32[2,2,32,128]{3,2,1,0:T(8,128)S(1)}, f32[2,2,32,128]{3,2,1,0:T(8,128)S(1)}, u32[]{:S(2)}, u32[]{:S(2)}) collective-permute-start(f32[2,2,32,128]{3,2,1,0:T(8,128)S(1)} %get-tuple-element.32), channel_id=1, source_target_pairs={{0,17},{1,16},{8,25},{9,24},{16,1},{17,0},{24,9},{25,8},{2,19},{3,... | collective-permute-start | bytes 196616 | tf_op jit(solution)/shard_map/ppermute | solution.py:322
  17.2 4.0 %collective-permute-start.5 = (f32[2,2,32,128]{3,2,1,0:T(8,128)S(1)}, f32[2,2,32,128]{3,2,1,0:T(8,128)S(1)}, u32[]{:S(2)}, u32[]{:S(2)}) collective-permute-start(f32[2,2,32,128]{3,2,1,0:T(8,128)S(1)} %get-tuple-element.33), channel_id=1, source_target_pairs={{0,24},{1,25},{8,16},{9,17},{16,8},{17,9},{24,0},{25,1},{2,26},{3,... | collective-permute-start | bytes 196616 | tf_op jit(solution)/shard_map/ppermute | solution.py:322
  19.6 5.1 %collective-permute-start.6 = (f32[2,2,32,128]{3,2,1,0:T(8,128)S(1)}, f32[2,2,32,128]{3,2,1,0:T(8,128)S(1)}, u32[]{:S(2)}, u32[]{:S(2)}) collective-permute-start(f32[2,2,32,128]{3,2,1,0:T(8,128)S(1)} %get-tuple-element.34), channel_id=1, source_target_pairs={{0,25},{1,24},{8,17},{9,16},{16,9},{17,8},{24,1},{25,0},{2,27},{3,... | collective-permute-start | bytes 196616 | tf_op jit(solution)/shard_map/ppermute | solution.py:322
  24.7 17.3 %collective-permute-start.7 = (f32[8,2,32,128]{3,2,1,0:T(8,128)S(1)}, f32[8,2,32,128]{3,2,1,0:T(8,128)S(1)}, u32[]{:S(2)}, u32[]{:S(2)}) collective-permute-start(f32[8,2,32,128]{3,2,1,0:T(8,128)S(1)} %get-tuple-element.35), channel_id=1, source_target_pairs={{0,6},{2,4},{4,2},{6,0},{1,7},{3,5},{5,3},{7,1},{8,14},{10,12},{12... | collective-permute-start | bytes 786440 | tf_op jit(solution)/shard_map/ppermute | solution.py:286
  26.8 4.3 %collective-permute-start.14 = (f32[2,2,32,128]{3,2,1,0:T(8,128)S(1)}, f32[2,2,32,128]{3,2,1,0:T(8,128)S(1)}, u32[]{:S(2)}, u32[]{:S(2)}) collective-permute-start(f32[2,2,32,128]{3,2,1,0:T(8,128)S(1)} %get-tuple-element.42), channel_id=1, source_target_pairs={{0,1},{1,0},{8,9},{9,8},{16,17},{17,16},{24,25},{25,24},{2,3},{3,2... | collective-permute-start | bytes 196616 | tf_op jit(solution)/shard_map/ppermute | solution.py:322
  28.7 4.2 %collective-permute-start.15 = (f32[2,2,32,128]{3,2,1,0:T(8,128)S(1)}, f32[2,2,32,128]{3,2,1,0:T(8,128)S(1)}, u32[]{:S(2)}, u32[]{:S(2)}) collective-permute-start(f32[2,2,32,128]{3,2,1,0:T(8,128)S(1)} %get-tuple-element.43), channel_id=1, source_target_pairs={{0,9},{1,8},{8,1},{9,0},{16,25},{17,24},{24,17},{25,16},{2,11},{3,... | collective-permute-start | bytes 196616 | tf_op jit(solution)/shard_map/ppermute | solution.py:322
  28.7 5.4 %collective-permute-start.16 = (f32[2,2,32,128]{3,2,1,0:T(8,128)S(1)}, f32[2,2,32,128]{3,2,1,0:T(8,128)S(1)}, u32[]{:S(2)}, u32[]{:S(2)}) collective-permute-start(f32[2,2,32,128]{3,2,1,0:T(8,128)S(1)} %get-tuple-element.44), channel_id=1, source_target_pairs={{0,17},{1,16},{8,25},{9,24},{16,1},{17,0},{24,9},{25,8},{2,19},{3,... | collective-permute-start | bytes 196616 | tf_op jit(solution)/shard_map/ppermute | solution.py:322
  31.1 7.6 %collective-permute-start.11 = (f32[2,2,32,128]{3,2,1,0:T(8,128)S(1)}, f32[2,2,32,128]{3,2,1,0:T(8,128)S(1)}, u32[]{:S(2)}, u32[]{:S(2)}) collective-permute-start(f32[2,2,32,128]{3,2,1,0:T(8,128)S(1)} %get-tuple-element.39), channel_id=1, source_target_pairs={{0,8},{1,9},{8,0},{9,1},{16,24},{17,25},{24,16},{25,17},{2,10},{3,... | collective-permute-start | bytes 196616 | tf_op jit(solution)/shard_map/ppermute | solution.py:322
  33.0 4.7 %collective-permute-start.17 = (f32[2,2,32,128]{3,2,1,0:T(8,128)S(1)}, f32[2,2,32,128]{3,2,1,0:T(8,128)S(1)}, u32[]{:S(2)}, u32[]{:S(2)}) collective-permute-start(f32[2,2,32,128]{3,2,1,0:T(8,128)S(1)} %get-tuple-element.45), channel_id=1, source_target_pairs={{0,25},{1,24},{8,17},{9,16},{16,9},{17,8},{24,1},{25,0},{2,27},{3,... | collective-permute-start | bytes 196616 | tf_op jit(solution)/shard_map/ppermute | solution.py:322
  34.1 5.4 %collective-permute-start.12 = (f32[2,2,32,128]{3,2,1,0:T(8,128)S(1)}, f32[2,2,32,128]{3,2,1,0:T(8,128)S(1)}, u32[]{:S(2)}, u32[]{:S(2)}) collective-permute-start(f32[2,2,32,128]{3,2,1,0:T(8,128)S(1)} %get-tuple-element.40), channel_id=1, source_target_pairs={{0,16},{1,17},{8,24},{9,25},{16,0},{17,1},{24,8},{25,9},{2,18},{3,... | collective-permute-start | bytes 196616 | tf_op jit(solution)/shard_map/ppermute | solution.py:322
  36.6 4.3 %collective-permute-start.13 = (f32[2,2,32,128]{3,2,1,0:T(8,128)S(1)}, f32[2,2,32,128]{3,2,1,0:T(8,128)S(1)}, u32[]{:S(2)}, u32[]{:S(2)}) collective-permute-start(f32[2,2,32,128]{3,2,1,0:T(8,128)S(1)} %get-tuple-element.41), channel_id=1, source_target_pairs={{0,24},{1,25},{8,16},{9,17},{16,8},{17,9},{24,0},{25,1},{2,26},{3,... | collective-permute-start | bytes 196616 | tf_op jit(solution)/shard_map/ppermute | solution.py:322
